TPU v7x, 32 devices: a 4x4x1 block of a 4x4x8 slice. The times are simulated.
32 devices in a mesh: dp: 1 (over z), ep: 32 (over y, x, core).
Axes of the slice: x: 4, y: 4, z: 1, core: 2. Of those that a mesh axis runs over, the one named last changes fastest.
The devices are a block of a 4x4x8 slice.
Arguments:
- tokens: bfloat16 [8192, 1536], P(('dp', 'ep'))
- expert_ids: int32 [8192, 6], P(('dp', 'ep'))
- gate_vals: float32 [8192, 6], P(('dp', 'ep'))
- w_gate: bfloat16 [64, 1536, 512], P('ep')
- w_up: bfloat16 [64, 1536, 512], P('ep')
- w_down: bfloat16 [64, 512, 1536], P('ep')
- shared_gate: bfloat16 [1536, 1024], replicated
- shared_up: bfloat16 [1536, 1024], replicated
- shared_down: bfloat16 [1024, 1536], replicated
Outputs:
- output: bfloat16 [8192, 1536], P(('dp', 'ep'))
All inputs are finite; a program needn't handle non-finite values.
Results may differ from a plain program's by a relative error of at most 0.00669537.
Values are sent between devices in bfloat16 or wider.
A program may use at most 768 MiB of HBM per device.

v0:
```python
import jax
import jax.numpy as jnp
from jax import lax
from jax.sharding import PartitionSpec as P


def swiglu(row_block, gate_w, up_w, down_w):
    gate_act = jnp.dot(row_block, gate_w, preferred_element_type=jnp.float32)
    up_act = jnp.dot(row_block, up_w, preferred_element_type=jnp.float32)
    hidden = (jax.nn.silu(gate_act) * up_act).astype(jnp.bfloat16)
    return jnp.dot(hidden, down_w, preferred_element_type=jnp.float32).astype(jnp.bfloat16)


def expert_block(recv_buf, w_gate, w_up, w_down):
    gate_act = jnp.einsum("slcd,ldf->slcf", recv_buf, w_gate, preferred_element_type=jnp.float32)
    up_act = jnp.einsum("slcd,ldf->slcf", recv_buf, w_up, preferred_element_type=jnp.float32)
    hidden = (jax.nn.silu(gate_act) * up_act).astype(jnp.bfloat16)
    return jnp.einsum("slcf,lfd->slcd", hidden, w_down, preferred_element_type=jnp.float32).astype(jnp.bfloat16)


def solution(mesh):
    group_size = mesh.shape["ep"]

    def moe_step(tokens, expert_ids, gate_vals, w_gate, w_up, w_down, shared_gate, shared_up, shared_down):
        tok_count, model_dim = tokens.shape
        top_count = expert_ids.shape[1]
        local_count = w_gate.shape[0]
        expert_count = local_count * group_size
        spread = max(group_size, expert_count // 2)
        capacity = (tok_count * top_count + spread - 1) // spread
        flat_ids = expert_ids.reshape(-1)
        one_hot = (flat_ids[:, None] == jnp.arange(expert_count, dtype=jnp.int32)[None, :]).astype(jnp.int32)
        slot_pos = jnp.sum(jnp.cumsum(one_hot, axis=0) * one_hot, axis=1) - 1
        columns = (flat_ids * capacity + slot_pos).reshape(tok_count, top_count)
        col_range = jnp.arange(expert_count * capacity, dtype=jnp.int32)
        dispatch = jnp.any(columns[:, :, None] == col_range[None, None, :], axis=1).astype(jnp.bfloat16)
        send_buf = jnp.einsum("tn,td->nd", dispatch, tokens, preferred_element_type=jnp.float32).astype(jnp.bfloat16)
        recv_buf = lax.all_to_all(send_buf, "ep", 0, 0, tiled=True)
        expert_out = expert_block(recv_buf.reshape(group_size, local_count, capacity, model_dim), w_gate, w_up, w_down)
        back_buf = lax.all_to_all(expert_out.reshape(expert_count * capacity, model_dim), "ep", 0, 0, tiled=True)
        picked = jnp.take(back_buf, columns, axis=0)
        shared_out = swiglu(tokens, shared_gate, shared_up, shared_down)
        result_acc = tokens.astype(jnp.float32) + jnp.sum(gate_vals[:, :, None] * picked.astype(jnp.float32), axis=1)
        return (result_acc + shared_out.astype(jnp.float32)).astype(jnp.bfloat16)

    row_spec = P(("dp", "ep"), None)
    expert_spec = P("ep", None, None)
    whole_spec = P(None, None)
    return jax.shard_map(moe_step, mesh=mesh, in_specs=(row_spec, row_spec, row_spec, expert_spec, expert_spec, expert_spec, whole_spec, whole_spec, whole_spec), out_specs=row_spec, check_vma=False)
```

profile of v0, /device:TPU:103, one launch (start us, length us, event | category | flops | bytes accessed | tf_op | source)
XLA Modules:
  0.0 385.3 jit_solution(15363633142355894767)
XLA Ops:
  0.0 0.0 copy-start
  0.0 1.0 copy.34
  1.0 0.1 eq.42
  1.1 0.1 eq.38
  1.3 0.8 fusion.27
  2.1 34.5 %reduce-window.6 = s32[64,12,128]{2,1,0:T(8,128)} reduce-window(s32[64,12,128]{2,1,0:T(8,128)} %fusion.27, s32[]{:T(128)} %constant.21.clone.1), window={size=1x1x128 pad=0_0x0_0x127_0}, to_apply=%region_0.0 | reduce-window | flops 12484608 | bytes 786436 | tf_op jit(solution)/shard_map/reduce-window
  36.6 2.0 slice.10
  38.7 1.3 copy.36
  40.0 0.1 copy.37
  40.1 1.2 broadcast_add_fusion
  41.3 0.1 fusion.29
  41.5 0.1 sub.7
  41.6 0.1 copy.38
  41.7 0.7 compare_and_fusion
  42.4 4.2 %fusion = pred[256,3072]{1,0:T(8,128)(4,1)S(1)} fusion(s32[256,6]{0,1:T(8,128)S(1)} %get-tuple-element.6), kind=kLoop, calls=%fused_computation.2 | loop fusion | flops 8650752 | bytes 792576 | tf_op jit(solution)/shard_map/reduce_or | solution.py:36
  46.6 4.1 %convolution_convert_fusion = bf16[3072,1536]{1,0:T(8,128)(2,1)S(1)} fusion(pred[256,3072]{1,0:T(8,128)(4,1)S(1)} %fusion, bf16[256,1536]{1,0:T(8,128)(2,1)} %param.9), kind=kOutput, calls=%fused_computation.4 | convolution fusion | flops 2420637696 | bytes 11010048 | tf_op jit(solution)/shard_map/tn,td->nd/dot_general | solution.py:37
  50.7 121.6 %all_to_all.21 = bf16[32,96,1536]{2,1,0:T(8,128)(2,1)S(1)} all-to-all(bf16[32,96,1536]{2,1,0:T(8,128)(2,1)S(1)} %bitcast.66), channel_id=1, replica_groups=mesh['dp'=1,'ep'=32] {'ep'}, dimensions={0} | all-to-all | bytes 18874368 | tf_op jit(solution)/shard_map/all_to_all | solution.py:38
  172.3 3.7 copy-done.2
  175.9 8.8 %fusion.1 = f32[2,32,48,512]{3,2,1,0:T(8,128)} fusion(bf16[32,2,48,1536]{3,2,1,0:T(8,128)(2,1)S(1)} %bitcast.68, bf16[2,1536,512]{2,1,0:T(8,128)(2,1)} %param.13), kind=kOutput, calls=%fused_computation.6 | convolution fusion | flops 4831838208 | bytes 18874368 | tf_op jit(solution)/shard_map/slcd,ldf->slcf/dot_general | solution.py:16
  184.7 16.7 %convert_bitcast_fusion = bf16[32,2,48,1536]{3,2,0,1:T(8,128)(2,1)} fusion(f32[2,32,48,512]{3,2,1,0:T(8,128)} %fusion.1, bf16[2,512,1536]{2,1,0:T(8,128)(2,1)S(1)} %copy-done, bf16[32,2,48,1536]{3,2,1,0:T(8,128)(2,1)} %bitcast.69, bf16[2,1536,512]{2,1,0:T(8,128)(2,1)} %param.12), kind=kOutput, calls=%fused_computation.5 | convolution fusion | flops 9677832192 | bytes 31457280 | tf_op jit(solution)/shard_map/slcf,lfd->slcd/dot_general | solution.py:18
  201.5 8.2 %copy.42 = bf16[32,2,48,1536]{3,2,1,0:T(8,128)(2,1)} copy(bf16[32,2,48,1536]{3,2,0,1:T(8,128)(2,1)} %convert_bitcast_fusion) | data formatting | bytes 18874368 | tf_op jit(solution)/shard_map/convert_element_type | solution.py:18
  209.7 7.5 %all-to-all-start.1 = ((bf16[32,96,1536]{2,1,0:T(8,128)(2,1)}), bf16[32,96,1536]{2,1,0:T(8,128)(2,1)}, u32[]{:S(2)}, u32[]{:S(2)}) async-start(bf16[32,96,1536]{2,1,0:T(8,128)(2,1)} %bitcast.67), calls=%async_computation.1 | async-start | bytes 18874368 | tf_op jit(solution)/shard_map/all_to_all | solution.py:40
  217.2 0.1 copy.43
  217.3 0.1 reshape.49
  217.5 0.2 copy.39
  217.6 0.1 copy.33
  217.8 3.9 %fusion.32 = f32[256,1024]{1,0:T(8,128)} fusion(bf16[256,1536]{1,0:T(8,128)(2,1)S(1)} %copy-done.3, bf16[1536,1024]{1,0:T(8,128)(2,1)} %param.15), kind=kOutput, calls=%fused_computation.42 | convolution fusion | flops 805306368 | bytes 4980736 | tf_op jit(solution)/shard_map/dot_general | solution.py:8
  221.7 124.1 %all-to-all-done.1 = bf16[32,96,1536]{2,1,0:T(8,128)(2,1)} async-done(((bf16[32,96,1536]{2,1,0:T(8,128)(2,1)}), bf16[32,96,1536]{2,1,0:T(8,128)(2,1)}, u32[]{:S(2)}, u32[]{:S(2)}) %all-to-all-start.1) | async-done | bytes 9437216 | tf_op jit(solution)/shard_map/all_to_all | solution.py:40
  345.7 15.3 %gather_fusion = bf16[1536,1536]{1,0:T(8,128)(2,1)} fusion(bf16[3072,1536]{1,0:T(8,128)(2,1)} %bitcast.14, s32[2048]{0:T(1024)S(1)} %pad_clamp_fusion), kind=kCustom, calls=%fused_computation | custom fusion | bytes 9443328 | tf_op jit(solution)/shard_map/jit(_take)/gather | solution.py:41
  361.0 8.3 %reshape.48 = bf16[256,6,1536]{2,1,0:T(8,128)(2,1)} reshape(bf16[1536,1536]{1,0:T(8,128)(2,1)} %gather_fusion) | data formatting | bytes 9437184 | tf_op jit(solution)/shard_map/jit(_take)/gather | solution.py:41
  369.3 9.3 %multiply_reduce_fusion = f32[256,1536]{1,0:T(8,128)} fusion(bf16[256,6,1536]{2,1,0:T(8,128)(2,1)} %reshape.48, f32[256,6]{1,0:T(8,128)S(1)} %copy.33, pred[256,6]{1,0:T(8,128)(4,1)S(1)} %copy.39), kind=kLoop, calls=%fused_computation.3 | loop fusion | flops 9043968 | bytes 6299136 | tf_op jit(solution)/shard_map/reduce_sum | solution.py:43
  378.6 6.7 %fusion.16 = bf16[256,1536]{1,0:T(8,128)(2,1)} fusion(bf16[1024,1536]{1,0:T(8,128)(2,1)} %param.17, f32[256,1536]{1,0:T(8,128)} %multiply_reduce_fusion, bf16[256,1536]{1,0:T(8,128)(2,1)} %param.9, bf16[1536,1024]{1,0:T(8,128)(2,1)} %param.16, f32[256,1024]{1,0:T(8,128)} %fusion.32), kind=kOutput, calls=%fused_computation.24 | convolution fusion | flops 1614544896 | bytes 10485760 | tf_op jit(solution)/shard_map/dot_general | solution.py:11
  (12 shorter events, 0.1 us)
Async XLA Ops:
  0.0 184.7 %copy-start = (bf16[2,512,1536]{2,1,0:T(8,128)(2,1)S(1)}, bf16[2,512,1536]{2,1,0:T(8,128)(2,1)}, u32[]{:S(2)}) copy-start(bf16[2,512,1536]{2,1,0:T(8,128)(2,1)} %param.14) | copy-start | bytes 9437188
  172.3 3.7 copy-start.2
  209.7 8.0 %copy-start.4 = (f32[256,6]{0,1:T(8,128)S(1)}, f32[256,6]{0,1:T(8,128)}, u32[]{:S(2)}) copy-start(f32[256,6]{0,1:T(8,128)} %param.11) | copy-start | bytes 18436
  209.7 8.1 %copy-start.3 = (bf16[256,1536]{1,0:T(8,128)(2,1)S(1)}, bf16[256,1536]{1,0:T(8,128)(2,1)}, u32[]{:S(2)}) copy-start(bf16[256,1536]{1,0:T(8,128)(2,1)} %param.9) | copy-start | bytes 2359300
  209.7 136.0 %all-to-all-start.1 = ((bf16[32,96,1536]{2,1,0:T(8,128)(2,1)}), bf16[32,96,1536]{2,1,0:T(8,128)(2,1)}, u32[]{:S(2)}, u32[]{:S(2)}) async-start(bf16[32,96,1536]{2,1,0:T(8,128)(2,1)} %bitcast.67), calls=%async_computation.1 | async-start | bytes 18874368 | tf_op jit(solution)/shard_map/all_to_all | solution.py:40
  369.3 16.0 %copy-start.1 = (bf16[2,512,1536]{2,1,0:T(8,128)(2,1)S(1)}, bf16[2,512,1536]{2,1,0:T(8,128)(2,1)}, u32[]{:S(2)}) copy-start(bf16[2,512,1536]{2,1,0:T(8,128)(2,1)} %param.14) | copy-start | bytes 9437188
where the time goes:
time: 389 us; the launch traced here: 385 us
  waiting for transfers between devices  124 us (32%)
  blocking collectives  122 us (31%)
  other arithmetic  51 us (13%)
  local copies, waits for them, and re-layouts  40.9 us (11%)
  matrix products  40.1 us (10%)
  starting transfers between devices  7.46 us (2%)
    all_to_all x1, waiting for transfers between devices, moe_step(): lax.all_to_all(expert_out.reshape(expert_count * capacity, model_dim), 'e...  124 us
    all_to_all x1, blocking collectives, moe_step(): recv_buf = lax.all_to_all(send_buf, 'ep', 0, 0, tiled=True)  122 us
    another operation x3, other arithmetic  35.8 us
    gather x2, local copies, waits for them, and re-layouts, moe_step(): picked = jnp.take(back_buf, columns, axis=0)  23.6 us
    dot_general x1, matrix products, expert_block(): jnp.einsum('slcf,lfd->slcd', hidden, w_down, preferred_element_type=jnp.f...  16.7 us
    reduce_sum x1, other arithmetic, moe_step(): jnp.sum(gate_vals[:, :, None] * picked.astype(jnp.float32), axis=1)  9.31 us
    dot_general x1, matrix products, expert_block(): jnp.einsum('slcd,ldf->slcf', recv_buf, w_up, preferred_element_type=jnp.f...  8.76 us
    convert_element_type x1, local copies, waits for them, and re-layouts, expert_block(): jnp.einsum('slcf,lfd->slcd', hidden, w_down, preferred_element_type=jnp.f...  8.22 us
  transfers between devices with their start and end apart: 1, of which 1 were waited for; matrix products, arithmetic and copies ran while one was open for 1% of the time, Pallas kernels for 0%

commit v1 on v0

v1 whole, which is shorter than its diff:
```python
import functools
import math

import jax
import jax.numpy as jnp
from jax import lax
from jax.experimental import pallas as pl
from jax.experimental.pallas import tpu as pltpu
from jax.sharding import PartitionSpec as P

F32 = jnp.float32
BF16 = jnp.bfloat16
MESH = pl.DeviceIdType.MESH


OFFSETS = (0, -1, 1, 2)


def kernel(side, cap, ids_ref, gat_ref, tok_hbm, wg_hbm, wu_hbm, wd_hbm, sg_hbm, su_hbm, sd_hbm, out_ref,
           w_g, w_u, w_d, tok, info, xbuf, fbuf, raw, relay, gsplit, part, acc, half, fin,
           own_sem, tok_r, tu_s, fu_s, tv_s, fv_s, inf_r, iu_s, iv_s, raw_r, rel_r, f_s, rel_s,
           half_r, half_s, fin_r, fin_s, sh_sem, wl_sem, wr_s, wr_r):
    tok_count, model_dim = tok_hbm.shape
    top_count = ids_ref.shape[1]
    local_count, _, ff = wg_hbm.shape
    chip_experts = 2 * local_count
    block = chip_experts * cap
    piece = tok_count // 2
    hblock = block // 2

    me = lax.axis_index("ep")
    c = me % 2
    chip = me // 2
    cx, cy = chip % side, chip // side
    u = (1 - c) * cx + c * cy
    v = (1 - c) * cy + c * cx

    def chip_at(uu, vv):
        uu, vv = (uu + side) % side, (vv + side) % side
        return (1 - c) * (vv * side + uu) + c * (uu * side + vv)

    def dev_at(uu, vv):
        return chip_at(uu, vv) * 2 + c

    u_dev = (dev_at(u + 1, v), dev_at(u - 1, v))
    v_dev = (dev_at(u, v + 1), dev_at(u, v - 1))
    partner = chip * 2 + (1 - c)
    side_of = (1, 2)

    sent = []

    def send(src, dst, ssem, rsem, dev, keep=None):
        copy = pltpu.make_async_remote_copy(src_ref=src, dst_ref=dst, send_sem=ssem, recv_sem=rsem,
                                            device_id={"ep": dev}, device_id_type=MESH)
        copy.start()
        (sent if keep is None else keep).append(copy)

    def arrived(dst, rsem):
        pltpu.make_async_remote_copy(src_ref=dst, dst_ref=dst, send_sem=half_s.at[0], recv_sem=rsem,
                                     device_id={"ep": me}, device_id_type=MESH).wait_recv()

    def rows_of(p):
        return pl.ds(p * piece, piece)

    def tok_wait(g, k, p):
        arrived(tok.at[g, k, rows_of(p)], tok_r.at[g, k, p])

    own = pltpu.make_async_copy(tok_hbm, tok.at[0, 0], own_sem)
    own.start()
    shared_loads = []
    for i in range(local_count):
        cols = pl.ds(i * ff, ff)
        for j, (src, dst) in enumerate(((sg_hbm.at[:, cols], w_g), (su_hbm.at[:, cols], w_u), (sd_hbm.at[cols], w_d))):
            copy = pltpu.make_async_copy(src, dst.at[i], sh_sem.at[i, j])
            copy.start()
            shared_loads.append(copy)

    barrier = pltpu.get_barrier_semaphore()
    for dev in u_dev + v_dev + (partner,):
        pl.semaphore_signal(barrier, inc=1, device_id={"ep": dev}, device_id_type=MESH)
    pl.semaphore_wait(barrier, 5)

    own.wait()

    def send_u_own():
        for order in range(2):
            for d in range(2):
                p = (d + order) % 2
                send(tok.at[0, 0, rows_of(p)], tok.at[0, side_of[d], rows_of(p)], tu_s.at[d, p],
                     tok_r.at[0, side_of[d], p], u_dev[d])

    def send_v(k):
        for order in range(2):
            for d in range(2):
                p = (d + order) % 2
                send(tok.at[0, k, rows_of(p)], tok.at[side_of[d], k, rows_of(p)], tv_s.at[k, d, p],
                     tok_r.at[side_of[d], k, p], v_dev[d])

    def forward_u(d):
        tok_wait(0, side_of[d], d)
        send(tok.at[0, side_of[d], rows_of(d)], tok.at[0, 3, rows_of(d)], fu_s.at[d], tok_r.at[0, 3, d], u_dev[d])

    def forward_v(k, d):
        tok_wait(side_of[d], k, d)
        send(tok.at[side_of[d], k, rows_of(d)], tok.at[3, k, rows_of(d)], fv_s.at[k, d], tok_r.at[3, k, d], v_dev[d])

    send_u_own()
    send_v(0)
    for i in range(local_count):
        for j, (src, dst) in enumerate(((wg_hbm, w_g), (wu_hbm, w_u), (wd_hbm, w_d))):
            send(src.at[i], dst.at[local_count + i], wr_s.at[i, j], wr_r.at[i, j], partner)

    lane = lax.broadcasted_iota(jnp.int32, (tok_count, 128), 1)
    hots = []
    chosen = jnp.zeros((tok_count, 128), F32)
    for j in range(top_count):
        hot = (ids_ref[:, j:j + 1] == lane).astype(F32)
        hots.append(hot)
        chosen = chosen + hot
    below = (lax.broadcasted_iota(jnp.int32, (tok_count, tok_count), 0)
             > lax.broadcasted_iota(jnp.int32, (tok_count, tok_count), 1)).astype(F32).astype(BF16)
    slot = jnp.dot(below, chosen.astype(BF16), preferred_element_type=F32)
    table = jnp.zeros((tok_count, 128), F32)
    for j in range(top_count):
        code = ids_ref[:, j:j + 1].astype(F32) * cap + jnp.sum(hots[j] * slot, axis=1, keepdims=True)
        table = table + jnp.where(lane == j, code, 0.0) + jnp.where(lane == 8 + j, gat_ref[:, j:j + 1], 0.0)
    info[0, 0] = table.T[0:16]

    def silu_mul(g, up):
        return (jax.nn.silu(g) * up).astype(BF16)

    n_step = 512 if model_dim % 512 == 0 else model_dim

    def shared_part(i):
        for copy in shared_loads[3 * i:3 * i + 3]:
            copy.wait()
        x = tok[0, 0]
        h = silu_mul(jnp.dot(x, w_g[i], preferred_element_type=F32), jnp.dot(x, w_u[i], preferred_element_type=F32))
        for n in range(0, model_dim, n_step):
            y = jnp.dot(h, w_d[i, :, n:n + n_step], preferred_element_type=F32)
            if i > 0:
                y = y + acc[:, n:n + n_step]
            if i == local_count - 1:
                y = y.astype(BF16).astype(F32) + x[:, n:n + n_step].astype(F32)
            acc[:, n:n + n_step] = y

    own_loads = []

    def load_own(i):
        for j, (src, dst) in enumerate(((wg_hbm, w_g), (wu_hbm, w_u), (wd_hbm, w_d))):
            copy = pltpu.make_async_copy(src.at[i], dst.at[i], wl_sem.at[i, j])
            copy.start()
            own_loads.append(copy)

    shared_part(0)
    load_own(0)

    def inf_wait(g, k):
        arrived(info.at[g, k], inf_r.at[g, k])

    def info_v(k):
        for d in range(2):
            send(info.at[0, k], info.at[side_of[d], k], iv_s.at[k, d], inf_r.at[side_of[d], k], v_dev[d])

    for d in range(2):
        send(info.at[0, 0], info.at[0, side_of[d]], iu_s.at[d], inf_r.at[0, side_of[d]], u_dev[d])
    info_v(0)

    for i in range(1, local_count):
        shared_part(i)
        load_own(i)

    forward_u(0)
    forward_u(1)
    inf_wait(0, 1)
    send(info.at[0, 1], info.at[0, 3], iu_s.at[2], inf_r.at[0, 3], u_dev[0])
    inf_wait(0, 2)
    tok_wait(0, 1, 1)
    send_v(1)
    info_v(1)
    tok_wait(0, 2, 0)
    send_v(2)
    info_v(2)

    def pass_v(k):
        forward_v(k, 0)
        forward_v(k, 1)
        inf_wait(1, k)
        send(info.at[1, k], info.at[3, k], iv_s.at[k, 2], inf_r.at[3, k], v_dev[0])
        inf_wait(2, k)

    pass_v(0)
    tok_wait(0, 3, 0)
    tok_wait(0, 3, 1)
    inf_wait(0, 3)
    send_v(3)
    info_v(3)

    slot_rows = lax.broadcasted_iota(jnp.int32, (block, tok_count), 0)
    turned = (slot_rows + c * (local_count * cap)) % block

    def row_codes(chip_idx):
        return (turned + chip_idx * block).astype(F32)

    f_sent = [[] for _ in range(4)]

    def experts(g):
        slot_f = g % 2
        if g >= 2:
            for copy in f_sent[g - 2]:
                copy.wait_send()

        def pick(k, carry):
            codes = row_codes(chip)
            hit = jnp.zeros((block, tok_count), F32)
            for j in range(top_count):
                hit = hit + (info[g, k, j:j + 1, :] == codes).astype(F32)
            hit = hit.astype(BF16)
            for n in range(0, model_dim, n_step):
                x = jnp.dot(hit, tok[g, k, :, n:n + n_step], preferred_element_type=F32).astype(BF16)
                for e in range(chip_experts):
                    xbuf[e, pl.ds(pl.multiple_of(k * cap, 16), cap), n:n + n_step] = x[e * cap:(e + 1) * cap]
            return carry

        lax.fori_loop(0, 4, pick, 0)

        def one(e, carry):
            x = xbuf[e]
            h = silu_mul(jnp.dot(x, w_g[e], preferred_element_type=F32), jnp.dot(x, w_u[e], preferred_element_type=F32))
            at = pl.ds(pl.multiple_of(e * cap, 16), cap)
            for n in range(0, model_dim, n_step):
                y = jnp.dot(h, w_d[e, :, n:n + n_step], preferred_element_type=F32).astype(BF16)
                raw[g, at, n:n + n_step] = y[0:cap]
                for k in range(1, 4):
                    fbuf[slot_f, k - 1, at, n:n + n_step] = y[k * cap:(k + 1) * cap]
            return carry

        lax.fori_loop(0, chip_experts, one, 0)

    def hrows(p):
        return pl.ds(p * hblock, hblock)

    def raw_rows(m, p):
        return pl.ds(m * block + p * hblock, hblock)

    def send_rows(g):
        slot_f = g % 2
        for d in range(2):
            send(fbuf.at[slot_f, 2, hrows(d)], relay.at[g, d], f_s.at[g, d, 2], rel_r.at[g, d], u_dev[d], f_sent[g])
        for d in range(2):
            for p in range(2):
                send(fbuf.at[slot_f, 1 - d, hrows(p)], raw.at[g, raw_rows(side_of[d], p)], f_s.at[g, d, p],
                     raw_r.at[g, side_of[d] - 1, p], u_dev[d], f_sent[g])

    def pass_rows(g):
        for d in range(2):
            arrived(relay.at[g, d], rel_r.at[g, d])
            send(relay.at[g, d], raw.at[g, raw_rows(3, d)], rel_s.at[g, d], raw_r.at[g, 2, d], u_dev[d])

    def combine(g, store):
        for m in range(1, 4):
            for p in range(2):
                arrived(raw.at[g, raw_rows(m, p)], raw_r.at[g, m - 1, p])
        for m in range(4):
            codes = row_codes(chip_at(u + OFFSETS[m], v))
            gate = jnp.zeros((block, tok_count), F32)
            for j in range(top_count):
                gate = gate + jnp.where(info[g, 0, j:j + 1, :] == codes, info[g, 0, 8 + j:9 + j, :], 0.0)
            gate = gate.T
            for s in range(3):
                part_s = gate.astype(BF16)
                gsplit[s * tok_count:(s + 1) * tok_count, m * block:(m + 1) * block] = part_s
                gate = gate - part_s.astype(F32)
        step = 256 if model_dim % 256 == 0 else model_dim

        def cols(n, carry):
            at = pl.ds(pl.multiple_of(n * step, 128), step)
            y = jnp.dot(gsplit[...], raw[g, :, at], preferred_element_type=F32)
            store(at, y[0:tok_count] + y[tok_count:2 * tok_count] + y[2 * tok_count:3 * tok_count])
            return carry

        lax.fori_loop(0, model_dim // step, cols, 0)

    def store_own(at, y):
        acc[:, at] = acc[:, at] + y

    def store_part(g):
        def store(at, y):
            part[g - 1, :, at] = y
        return store

    def send_fin(g, d, p):
        send(part.at[g - 1, rows_of(p)], fin.at[d, rows_of(p)], fin_s.at[d, p], fin_r.at[d, p], v_dev[d])

    for copy in own_loads:
        copy.wait()
    for i in range(local_count):
        for j, dst in enumerate((w_g, w_u, w_d)):
            arrived(dst.at[local_count + i], wr_r.at[i, j])

    experts(0)
    pass_v(1)
    send_rows(0)
    pass_v(2)
    pass_v(3)
    for k in range(4):
        tok_wait(1, k, 1)
    experts(1)
    pass_rows(0)
    send_rows(1)
    for k in range(4):
        tok_wait(2, k, 0)
    experts(2)
    pass_rows(1)
    send_rows(2)
    combine(0, store_own)
    pass_rows(2)
    for k in range(4):
        tok_wait(3, k, 0)
        tok_wait(3, k, 1)
        inf_wait(3, k)
    experts(3)
    combine(1, store_part(1))
    send_rows(3)
    send_fin(1, 1, 0)
    combine(2, store_part(2))
    pass_rows(3)
    send_fin(2, 0, 1)
    combine(3, store_part(3))
    for d in range(2):
        send(part.at[2, rows_of(d)], half.at[d], half_s.at[d], half_r.at[d], v_dev[d])
    for d in range(2):
        g = 2 - d
        arrived(half.at[d], half_r.at[d])
        part[g - 1, d * piece:(d + 1) * piece] = part[g - 1, d * piece:(d + 1) * piece] + half[d]
        send_fin(g, d, d)
    for p in range(2):
        for d in range(2):
            arrived(fin.at[d, rows_of(p)], fin_r.at[d, p])
        at = slice(p * piece, (p + 1) * piece)
        out_ref[at] = (acc[at] + fin[0, at] + fin[1, at]).astype(out_ref.dtype)

    for copies in f_sent[2:] + [sent]:
        for copy in copies:
            copy.wait_send()


def solution(mesh):
    group_size = mesh.shape["ep"]
    side = math.isqrt(group_size // 2)

    def moe_step(tokens, expert_ids, gate_vals, w_gate, w_up, w_down, shared_gate, shared_up, shared_down):
        tok_count, model_dim = tokens.shape
        top_count = expert_ids.shape[1]
        local_count, _, ff = w_gate.shape
        expert_count = local_count * group_size
        spread = max(group_size, expert_count // 2)
        cap = (tok_count * top_count + spread - 1) // spread
        block = 2 * local_count * cap
        piece = tok_count // 2
        dma = pltpu.SemaphoreType.DMA
        vmem = pl.BlockSpec(memory_space=pltpu.VMEM)
        hbm = pl.BlockSpec(memory_space=pl.ANY)
        scratch = [
            pltpu.VMEM((2 * local_count, model_dim, ff), BF16),
            pltpu.VMEM((2 * local_count, model_dim, ff), BF16),
            pltpu.VMEM((2 * local_count, ff, model_dim), BF16),
            pltpu.VMEM((4, 4, tok_count, model_dim), BF16),
            pltpu.VMEM((4, 4, 16, tok_count), F32),
            pltpu.VMEM((2 * local_count, 4 * cap, model_dim), BF16),
            pltpu.VMEM((2, 3, block, model_dim), BF16),
            pltpu.VMEM((4, 4 * block, model_dim), BF16),
            pltpu.VMEM((4, 2, block // 2, model_dim), BF16),
            pltpu.VMEM((3 * tok_count, 4 * block), BF16),
            pltpu.VMEM((3, tok_count, model_dim), F32),
            pltpu.VMEM((tok_count, model_dim), F32),
            pltpu.VMEM((2, piece, model_dim), F32),
            pltpu.VMEM((2, tok_count, model_dim), F32),
            dma(()), dma((4, 4, 2)), dma((2, 2)), dma((2,)), dma((4, 2, 2)), dma((4, 2)),
            dma((4, 4)), dma((3,)), dma((4, 3)),
            dma((4, 3, 2)), dma((4, 2)), dma((4, 2, 3)), dma((4, 2)),
            dma((2,)), dma((2,)), dma((2, 2)), dma((2, 2)),
            dma((local_count, 3)), dma((local_count, 3)), dma((local_count, 3)), dma((local_count, 3)),
        ]
        return pl.pallas_call(
            functools.partial(kernel, side, cap),
            out_shape=jax.ShapeDtypeStruct(tokens.shape, tokens.dtype),
            in_specs=[vmem, vmem] + [hbm] * 7,
            out_specs=vmem,
            scratch_shapes=scratch,
            compiler_params=pltpu.CompilerParams(collective_id=0, has_side_effects=True, vmem_limit_bytes=67043328),
        )(expert_ids, gate_vals, tokens, w_gate, w_up, w_down, shared_gate, shared_up, shared_down)

    row_spec = P(("dp", "ep"), None)
    expert_spec = P("ep", None, None)
    whole_spec = P(None, None)
    return jax.shard_map(moe_step, mesh=mesh, in_specs=(row_spec, row_spec, row_spec, expert_spec, expert_spec, expert_spec, whole_spec, whole_spec, whole_spec), out_specs=row_spec, check_vma=False)
```

time: 389 us -> 172 us (0.44)
  the two profiles are of different devices: /device:TPU:103 before, /device:TPU:97 now
where the time goes in v1:
time: 172 us; the launch traced here: 169 us
  Pallas kernels  164 us (95%)
  local copies, waits for them, and re-layouts  5.04 us (3%)
    pallas_call x1, Pallas kernels, moe_step(): pl.pallas_call(functools.partial(kernel, side, cap), out_shape=jax.ShapeD...  164 us
    unnamed x3, local copies, waits for them, and re-layouts  5.04 us

profile of v1, /device:TPU:97, one launch (start us, length us, event | category | flops | bytes accessed | tf_op | source)
XLA Modules:
  0.0 169.4 jit_solution(16297889850242575579)
XLA Ops:
  0.0 1.5 copy.10.ids_ref
  1.5 1.5 copy.11.gat_ref
  3.0 164.3 %shard_map.91 = bf16[256,1536]{1,0:T(8,128)(2,1)} custom-call(s32[256,6]{1,0:T(8,128)} %copy.10.ids_ref, f32[256,6]{1,0:T(8,128)} %copy.11.gat_ref, bf16[256,1536]{1,0:T(8,128)(2,1)} %tok_hbm.1, bf16[2,1536,512]{2,1,0:T(8,128)(2,1)} %wg_hbm.1, bf16[2,1536,512]{2,1,0:T(8,128)(2,1)} %wu_hbm.1, bf16[2,512,1536]{2,1,0:T(8,128)(2,1)} %wd_hbm.1, ...), custom_call_target="tpu_custom_call" | custom-call | tf_op jit(solution)/shard_map/pallas_call | solution.py:385
  167.3 2.1 %copy.13 = bf16[256,1536]{1,0:T(8,128)(2,1)} copy(bf16[256,1536]{1,0:T(8,128)(2,1)} %shard_map.91) | data formatting | bytes 1572864

commit v2 on v1

v2 whole, which is shorter than its diff:
```python
import functools
import math

import jax
import jax.numpy as jnp
from jax import lax
from jax.experimental import pallas as pl
from jax.experimental.pallas import tpu as pltpu
from jax.sharding import PartitionSpec as P

F32 = jnp.float32
BF16 = jnp.bfloat16
MESH = pl.DeviceIdType.MESH


OFFSETS = (0, -1, 1, 2)
SIDE = (1, 2)

WHOLE = {(0, 0): 0, (0, 1): 1, (0, 2): 2, (0, 3): 3, (1, 0): 4, (1, 2): 5, (2, 1): 6, (2, 3): 7}


def kernel(side, cap, ids_ref, gat_ref, tok_hbm, wg_hbm, wu_hbm, wd_hbm, sg_hbm, su_hbm, sd_hbm, out_ref,
           w_g, w_u, w_d, tok, info, xg, stage, raw, relay, gsplit, part, acc, half, fin,
           own_sem, tok_r, tu_s, fu_s, tv_s, x_r, xc_s, xf_s, inf_r, iu_s, iv_s, if_s, raw_r, rel_r, f_s, rel_s,
           half_r, half_s, fin_r, fin_s, sh_sem, wl_sem, wr_s, wr_r):
    tok_count, model_dim = tok_hbm.shape
    top_count = ids_ref.shape[0]
    local_count, _, ff = wg_hbm.shape
    chip_experts = 2 * local_count
    expert_count = local_count * side * side * 2
    block = chip_experts * cap
    piece = tok_count // 2
    chunks = 2
    width = model_dim // chunks

    me = lax.axis_index("ep")
    c = me % 2
    chip = me // 2
    cx, cy = chip % side, chip // side
    u = (1 - c) * cx + c * cy
    v = (1 - c) * cy + c * cx

    def chip_at(uu, vv):
        uu, vv = (uu + side) % side, (vv + side) % side
        return (1 - c) * (vv * side + uu) + c * (uu * side + vv)

    def dev_at(uu, vv):
        return chip_at(uu, vv) * 2 + c

    u_dev = (dev_at(u + 1, v), dev_at(u - 1, v))
    v_dev = (dev_at(u, v + 1), dev_at(u, v - 1))
    v_chip = (chip_at(u, v + 1), chip_at(u, v - 1))
    partner = chip * 2 + (1 - c)

    sent = []

    def send(src, dst, ssem, rsem, dev, keep=True):
        copy = pltpu.make_async_remote_copy(src_ref=src, dst_ref=dst, send_sem=ssem, recv_sem=rsem,
                                            device_id={"ep": dev}, device_id_type=MESH)
        copy.start()
        if keep:
            sent.append(copy)
        return copy

    def arrived(dst, rsem):
        pltpu.make_async_remote_copy(src_ref=dst, dst_ref=dst, send_sem=half_s.at[0, 0], recv_sem=rsem,
                                     device_id={"ep": me}, device_id_type=MESH).wait_recv()

    def rows_of(p):
        return pl.ds(p * piece, piece)

    own = pltpu.make_async_copy(tok_hbm, tok.at[0], own_sem)
    own.start()
    shared_loads = []
    for i in range(local_count):
        cols = pl.ds(i * ff, ff)
        for j, (src, dst) in enumerate(((sg_hbm.at[:, cols], w_g), (su_hbm.at[:, cols], w_u), (sd_hbm.at[cols], w_d))):
            copy = pltpu.make_async_copy(src, dst.at[i], sh_sem.at[i, j])
            copy.start()
            shared_loads.append(copy)

    barrier = pltpu.get_barrier_semaphore()
    for dev in u_dev + v_dev + (partner,):
        pl.semaphore_signal(barrier, inc=1, device_id={"ep": dev}, device_id_type=MESH)
    pl.semaphore_wait(barrier, 5)
    own.wait()

    def tok_wait(g, k, p):
        arrived(tok.at[WHOLE[g, k], rows_of(p)], tok_r.at[WHOLE[g, k], p])

    def send_u_own():
        for order in range(2):
            for d in range(2):
                p = (d + order) % 2
                send(tok.at[0, rows_of(p)], tok.at[SIDE[d], rows_of(p)], tu_s.at[d, p], tok_r.at[SIDE[d], p], u_dev[d])

    def forward_u(d):
        tok_wait(0, SIDE[d], d)
        send(tok.at[SIDE[d], rows_of(d)], tok.at[3, rows_of(d)], fu_s.at[d], tok_r.at[3, d], u_dev[d])

    def whole_v(k, p):
        d = k % 2
        at = WHOLE[SIDE[d], k]
        send(tok.at[k, rows_of(p)], tok.at[at, rows_of(p)], tv_s.at[k, p], tok_r.at[at, p], v_dev[d])

    send_u_own()
    whole_v(0, 0)
    whole_v(0, 1)

    expert = lax.broadcasted_iota(jnp.int32, (expert_count, tok_count), 0)
    hots = []
    chosen = jnp.zeros((expert_count, tok_count), F32)
    for j in range(top_count):
        hot = (ids_ref[j:j + 1, :] == expert).astype(F32)
        hots.append(hot)
        chosen = chosen + hot
    above = (lax.broadcasted_iota(jnp.int32, (tok_count, tok_count), 0)
             < lax.broadcasted_iota(jnp.int32, (tok_count, tok_count), 1)).astype(F32).astype(BF16)
    slot = jnp.dot(chosen.astype(BF16), above, preferred_element_type=F32)
    info[0, 0] = jnp.zeros((16, tok_count), F32)
    for j in range(top_count):
        info[0, 0, j:j + 1, :] = ids_ref[j:j + 1, :].astype(F32) * cap + jnp.sum(hots[j] * slot, axis=0, keepdims=True)
        info[0, 0, 8 + j:9 + j, :] = gat_ref[j:j + 1, :]

    slot_rows = lax.broadcasted_iota(jnp.int32, (block, tok_count), 0) + c * (local_count * cap)
    turned = jnp.where(slot_rows >= block, slot_rows - block, slot_rows)
    n_step = 512 if model_dim % 512 == 0 else model_dim

    def row_codes(chip_idx):
        return (turned + chip_idx * block).astype(F32)

    def pick(g, k, chip_idx, dst, first):
        codes = row_codes(chip_idx)
        hit = jnp.zeros((block, tok_count), F32)
        for j in range(top_count):
            hit = hit + (info[g, k, j:j + 1, :] == codes).astype(F32)
        hit = hit.astype(BF16)
        for n in range(0, model_dim, n_step):
            x = jnp.dot(hit, tok[WHOLE[g, k], :, n:n + n_step], preferred_element_type=F32).astype(BF16)
            for e in range(chip_experts):
                dst[e, first:first + cap, n:n + n_step] = x[e * cap:(e + 1) * cap]

    def group_rows(k):
        return pl.ds(k * cap, cap)

    near = [None] * 4

    def near_v(k):
        d = 1 - k % 2
        pick(0, k, v_chip[d], stage.at[k], 0)
        near[k] = send(stage.at[k], xg.at[SIDE[d], :, group_rows(k)], xc_s.at[k], x_r.at[SIDE[d], k], v_dev[d], False)

    def inf_wait(g, k):
        arrived(info.at[g, k], inf_r.at[g, k])

    def far_v(k):
        d = k % 2
        g = SIDE[d]
        tok_wait(g, k, 0)
        tok_wait(g, k, 1)
        inf_wait(g, k)
        near[k].wait_send()
        pick(g, k, v_chip[d], stage.at[k], 0)
        send(stage.at[k], xg.at[3, :, group_rows(k)], xf_s.at[k], x_r.at[3, k], v_dev[d])
        if k == 0:
            send(info.at[g, 0], info.at[3, 0], if_s, inf_r.at[3, 0], v_dev[d])

    def info_v(k):
        for d in range(2):
            if k == 0 or d == k % 2:
                send(info.at[0, k], info.at[SIDE[d], k], iv_s.at[k, d], inf_r.at[SIDE[d], k], v_dev[d])

    near_v(0)
    for d in range(2):
        send(info.at[0, 0], info.at[0, SIDE[d]], iu_s.at[d], inf_r.at[0, SIDE[d]], u_dev[d])
    info_v(0)

    for i in range(local_count):
        for j, (src, dst) in enumerate(((wg_hbm, w_g), (wu_hbm, w_u), (wd_hbm, w_d))):
            send(src.at[i], dst.at[local_count + i], wr_s.at[i, j], wr_r.at[i, j], partner)

    def silu_mul(g, up):
        return (jax.nn.silu(g) * up).astype(BF16)

    def shared_part(i):
        for copy in shared_loads[3 * i:3 * i + 3]:
            copy.wait()
        x = tok[0]
        h = silu_mul(jnp.dot(x, w_g[i], preferred_element_type=F32), jnp.dot(x, w_u[i], preferred_element_type=F32))
        for n in range(0, model_dim, n_step):
            y = jnp.dot(h, w_d[i, :, n:n + n_step], preferred_element_type=F32)
            if i > 0:
                y = y + acc[:, n:n + n_step]
            if i == local_count - 1:
                y = y.astype(BF16).astype(F32) + x[:, n:n + n_step].astype(F32)
            acc[:, n:n + n_step] = y

    own_loads = []

    def load_own(i):
        for j, (src, dst) in enumerate(((wg_hbm, w_g), (wu_hbm, w_u), (wd_hbm, w_d))):
            copy = pltpu.make_async_copy(src.at[i], dst.at[i], wl_sem.at[i, j])
            copy.start()
            own_loads.append(copy)

    for i in range(local_count):
        shared_part(i)
        load_own(i)

    forward_u(0)
    forward_u(1)
    inf_wait(0, 1)
    send(info.at[0, 1], info.at[0, 3], iu_s.at[2], inf_r.at[0, 3], u_dev[0])
    inf_wait(0, 2)
    whole_v(1, 0)
    whole_v(2, 1)
    tok_wait(0, 1, 1)
    whole_v(1, 1)
    info_v(1)
    near_v(1)
    tok_wait(0, 2, 0)
    whole_v(2, 0)
    info_v(2)
    near_v(2)
    far_v(0)
    for p in range(2):
        tok_wait(0, 3, p)
        whole_v(3, p)
    inf_wait(0, 3)
    info_v(3)
    near_v(3)

    def experts(g):
        def one(e, carry):
            x = xg[g, e]
            h = silu_mul(jnp.dot(x, w_g[e], preferred_element_type=F32), jnp.dot(x, w_u[e], preferred_element_type=F32))
            for n in range(0, model_dim, n_step):
                y = jnp.dot(h, w_d[e, :, n:n + n_step], preferred_element_type=F32).astype(BF16)
                raw[g, 0, e, :, n:n + n_step] = y[0:cap]
                xg[g, e, cap:4 * cap, n:n + n_step] = y[cap:4 * cap]
            return carry

        lax.fori_loop(0, chip_experts, one, 0)

    def own_pick(g, ks):
        for k in ks:
            pick(g, k, chip, xg.at[g], k * cap)

    def x_wait(g, ks):
        for k in ks:
            arrived(xg.at[g, :, group_rows(k)], x_r.at[g, k])

    def e_half(d):
        return pl.ds(d * local_count, local_count)

    def col_chunk(f):
        return slice(None) if f is None else pl.ds(f * width, width)

    def send_rows(g, f=None):
        at = col_chunk(f)
        i = f or 0
        for d in range(2):
            send(xg.at[g, e_half(d), group_rows(3), at], relay.at[g, d, :, :, at], f_s.at[g, d, 1, i],
                 rel_r.at[g, d, i], u_dev[d])
        for d in range(2):
            send(xg.at[g, :, group_rows(2 - d), at], raw.at[g, SIDE[d], :, :, at], f_s.at[g, d, 0, i],
                 raw_r.at[g, SIDE[d], 0, i], u_dev[d])

    def pass_rows(g, f=None):
        at = col_chunk(f)
        i = f or 0
        for d in range(2):
            arrived(relay.at[g, d, :, :, at], rel_r.at[g, d, i])
            send(relay.at[g, d, :, :, at], raw.at[g, 3, e_half(d), :, at], rel_s.at[g, d, i], raw_r.at[g, 3, d, i], u_dev[d])

    def raw_wait(g, f=None):
        at = col_chunk(f)
        i = f or 0
        for m in range(1, 3):
            arrived(raw.at[g, m, :, :, at], raw_r.at[g, m, 0, i])
        for d in range(2):
            arrived(raw.at[g, 3, e_half(d), :, at], raw_r.at[g, 3, d, i])

    def gates_of(g):
        for m in range(4):
            codes = row_codes(chip_at(u + OFFSETS[m], v))
            gate = jnp.zeros((block, tok_count), F32)
            for j in range(top_count):
                gate = gate + jnp.where(info[g, 0, j:j + 1, :] == codes, info[g, 0, 8 + j:9 + j, :], 0.0)
            gate = gate.T
            for s in range(3):
                part_s = gate.astype(BF16)
                gsplit[s * tok_count:(s + 1) * tok_count, m * block:(m + 1) * block] = part_s
                gate = gate - part_s.astype(F32)

    step = 256 if width % 256 == 0 else width

    def gated(g, f=None):
        first, count = (0, model_dim // step) if f is None else (f * (width // step), width // step)

        def cols(n, carry):
            at = pl.ds(pl.multiple_of(n * step, 128), step)
            rows = raw[g, :, :, :, at].reshape(4 * block, step)
            y = jnp.dot(gsplit[...], rows, preferred_element_type=F32)
            y = y[0:tok_count] + y[tok_count:2 * tok_count] + y[2 * tok_count:3 * tok_count]
            if g == 0:
                acc[:, at] = acc[:, at] + y
            else:
                part[g - 1, :, at] = y
            return carry

        lax.fori_loop(first, first + count, cols, 0)

    def send_fin(g, d, p, f=None):
        at = col_chunk(f)
        send(part.at[g - 1, rows_of(p), at], fin.at[d, rows_of(p), at], fin_s.at[d, p, f or 0], fin_r.at[d, p, f or 0], v_dev[d])

    own_pick(0, range(4))
    for copy in own_loads:
        copy.wait()
    for i in range(local_count):
        for j, dst in enumerate((w_g, w_u, w_d)):
            arrived(dst.at[local_count + i], wr_r.at[i, j])
    experts(0)
    far_v(1)
    send_rows(0)
    far_v(2)
    far_v(3)
    own_pick(1, (0, 2))
    x_wait(1, (1, 3))
    experts(1)
    pass_rows(0)
    send_rows(1)
    own_pick(2, (1, 3))
    x_wait(2, (0, 2))
    experts(2)
    pass_rows(1)
    send_rows(2)
    raw_wait(0)
    gates_of(0)
    gated(0)
    pass_rows(2)
    x_wait(3, range(4))
    experts(3)
    for f in range(chunks):
        send_rows(3, f)
    raw_wait(1)
    gates_of(1)
    gated(1)
    raw_wait(2)
    inf_wait(2, 0)
    gates_of(2)
    pass_rows(3, 0)
    gated(2)
    for f in range(1, chunks):
        pass_rows(3, f)
    inf_wait(3, 0)
    gates_of(3)
    for f in range(chunks):
        raw_wait(3, f)
        gated(3, f)
        for d in range(2):
            send(part.at[2, rows_of(d), col_chunk(f)], half.at[d, :, col_chunk(f)], half_s.at[d, f], half_r.at[d, f], v_dev[d])
    send_fin(1, 1, 0)
    send_fin(2, 0, 1)
    for f in range(chunks):
        at = slice(f * width, (f + 1) * width)
        for d in range(2):
            g = 2 - d
            arrived(half.at[d, :, col_chunk(f)], half_r.at[d, f])
            rows = slice(d * piece, (d + 1) * piece)
            part[g - 1, rows, at] = part[g - 1, rows, at] + half[d, :, at]
            send_fin(g, d, d, f)
    for d in range(2):
        arrived(fin.at[d, rows_of(1 - d)], fin_r.at[d, 1 - d, 0])
        rows = slice((1 - d) * piece, (2 - d) * piece)
        acc[rows] = acc[rows] + fin[d, rows]
    for f in range(chunks):
        at = slice(f * width, (f + 1) * width)
        for d in range(2):
            arrived(fin.at[d, rows_of(d), col_chunk(f)], fin_r.at[d, d, f])
            rows = slice(d * piece, (d + 1) * piece)
            out_ref[rows, at] = (acc[rows, at] + fin[d, rows, at]).astype(out_ref.dtype)

    for copy in sent:
        copy.wait_send()


def solution(mesh):
    group_size = mesh.shape["ep"]
    side = math.isqrt(group_size // 2)

    def moe_step(tokens, expert_ids, gate_vals, w_gate, w_up, w_down, shared_gate, shared_up, shared_down):
        tok_count, model_dim = tokens.shape
        top_count = expert_ids.shape[1]
        local_count, _, ff = w_gate.shape
        expert_count = local_count * group_size
        spread = max(group_size, expert_count // 2)
        cap = (tok_count * top_count + spread - 1) // spread
        block = 2 * local_count * cap
        piece = tok_count // 2
        dma = pltpu.SemaphoreType.DMA
        vmem = pl.BlockSpec(memory_space=pltpu.VMEM)
        hbm = pl.BlockSpec(memory_space=pl.ANY)
        scratch = [
            pltpu.VMEM((2 * local_count, model_dim, ff), BF16),
            pltpu.VMEM((2 * local_count, model_dim, ff), BF16),
            pltpu.VMEM((2 * local_count, ff, model_dim), BF16),
            pltpu.VMEM((len(WHOLE), tok_count, model_dim), BF16),
            pltpu.VMEM((4, 4, 16, tok_count), F32),
            pltpu.VMEM((4, 2 * local_count, 4 * cap, model_dim), BF16),
            pltpu.VMEM((4, 2 * local_count, cap, model_dim), BF16),
            pltpu.VMEM((4, 4, 2 * local_count, cap, model_dim), BF16),
            pltpu.VMEM((4, 2, local_count, cap, model_dim), BF16),
            pltpu.VMEM((3 * tok_count, 4 * block), BF16),
            pltpu.VMEM((3, tok_count, model_dim), F32),
            pltpu.VMEM((tok_count, model_dim), F32),
            pltpu.VMEM((2, piece, model_dim), F32),
            pltpu.VMEM((2, tok_count, model_dim), F32),
            dma(()), dma((len(WHOLE), 2)), dma((2, 2)), dma((2,)), dma((4, 2)), dma((4, 4)), dma((4,)), dma((4,)),
            dma((4, 4)), dma((3,)), dma((4, 2)), dma(()),
            dma((4, 4, 2, 2)), dma((4, 2, 2)), dma((4, 2, 2, 2)), dma((4, 2, 2)),
            dma((2, 2)), dma((2, 2)), dma((2, 2, 2)), dma((2, 2, 2)),
            dma((local_count, 3)), dma((local_count, 3)), dma((local_count, 3)), dma((local_count, 3)),
        ]
        return pl.pallas_call(
            functools.partial(kernel, side, cap),
            out_shape=jax.ShapeDtypeStruct(tokens.shape, tokens.dtype),
            in_specs=[vmem, vmem] + [hbm] * 7,
            out_specs=vmem,
            scratch_shapes=scratch,
            compiler_params=pltpu.CompilerParams(collective_id=0, has_side_effects=True, vmem_limit_bytes=67043328),
        )(expert_ids.T, gate_vals.T, tokens, w_gate, w_up, w_down, shared_gate, shared_up, shared_down)

    row_spec = P(("dp", "ep"), None)
    expert_spec = P("ep", None, None)
    whole_spec = P(None, None)
    return jax.shard_map(moe_step, mesh=mesh, in_specs=(row_spec, row_spec, row_spec, expert_spec, expert_spec, expert_spec, whole_spec, whole_spec, whole_spec), out_specs=row_spec, check_vma=False)
```

time: 172 us -> 152 us (0.88); the launches traced: 169 us -> 152 us
  Pallas kernels: 164 us -> 150 us
  local copies, waits for them, and re-layouts: 5.04 us -> 2.06 us
    pallas_call x1, Pallas kernels: 164 us -> 150 us  [moe_step(): pl.pallas_call(functools.partial(kernel, side, cap), out_shape=jax.ShapeD...]
    unnamed x3 -> x1, local copies, waits for them, and re-layouts: 5.04 us -> 2.06 us
where the time goes in v2:
time: 152 us
  Pallas kernels  150 us (99%)
  local copies, waits for them, and re-layouts  2.06 us (1%)
    pallas_call x1, Pallas kernels, moe_step(): pl.pallas_call(functools.partial(kernel, side, cap), out_shape=jax.ShapeD...  150 us

profile of v2, /device:TPU:97, one launch (start us, length us, event | category | flops | bytes accessed | tf_op | source)
XLA Modules:
  0.0 151.7 jit_solution(17084377683044543721)
XLA Ops:
  0.0 149.6 %shard_map.91 = bf16[256,1536]{1,0:T(8,128)(2,1)} custom-call(s32[6,256]{1,0:T(8,128)} %bitcast.2, f32[6,256]{1,0:T(8,128)} %bitcast.3, bf16[256,1536]{1,0:T(8,128)(2,1)} %tok_hbm.1, bf16[2,1536,512]{2,1,0:T(8,128)(2,1)} %wg_hbm.1, bf16[2,1536,512]{2,1,0:T(8,128)(2,1)} %wu_hbm.1, bf16[2,512,1536]{2,1,0:T(8,128)(2,1)} %wd_hbm.1, bf16[1536,1024]{1,0:T(8,128)(2,1)} %sg_hbm.1, ...), custom_call_target="tpu_custom_call" | custom-call | tf_op jit(solution)/shard_map/pallas_call | solution.py:426
  149.6 2.1 %copy.11 = bf16[256,1536]{1,0:T(8,128)(2,1)} copy(bf16[256,1536]{1,0:T(8,128)(2,1)} %shard_map.91) | data formatting | bytes 1572864
